TPU v7x, 32 devices: a whole 2x2x4 slice. The times are simulated.
32 devices in a mesh: dom: 8 (over z, y), orb: 4 (over x, core).
Axes of the slice: x: 2, y: 2, z: 4, core: 2. Of those that a mesh axis runs over, the one named last changes fastest.
Arguments:
- orbitals: bfloat16 [16, 4, 1024, 512], P('dom', None, None, 'orb'), may hold values from -6 to 6
- slot_ids: int32 [16, 4], P('dom'), may hold values from 0 to 15, as said below
- slot_count: int32 [16], P('dom'), may hold values from 1 to 4, as said below
- band_tiles: bfloat16 [16, 3, 512, 512], P(None, None, 'dom', 'orb'), may hold values from -0.15625 to 0.15625
- pattern: int32 [16, 3], replicated, may hold values 0 or 1
- occupation: float32 [16, 512], P(None, 'orb'), may hold values from 0.0005 to 0.005
Outputs:
- rotated: bfloat16 [16, 4, 1024, 512], P('dom', None, None, 'orb')
- density: float32 [16, 1024], P('dom')
Inputs may be any that keep to these rules, and one draw needn't show every extreme that they name: `slot_ids`: each row names 4 consecutive orbital blocks counted modulo 16: slot l holds (s + l) mod 16, where the first block s of a grid block may be any of the 16 blocks. The slots in use on grid block g are its first slot_count[g]; some grid block uses all 4.
All inputs are finite; a program needn't handle non-finite values.
Results may differ from a plain program's by a relative error of at most 0.00094.
Values may be sent and summed in bfloat16 or wider, within the bound.
A program may use at most 128 MiB of HBM per device.

v0:
```python
import jax
import jax.numpy as jnp
from jax import lax
from jax.sharding import PartitionSpec as P


def select_tiles(band_full, pattern, slot_ids, slot_count):
    slots_per = slot_ids.shape[1]
    band_count = pattern.shape[1]
    half_band = (band_count - 1) // 2
    active = jnp.arange(slots_per, dtype=jnp.int32)[None, :] < slot_count[:, None]
    source = slot_ids[:, :, None]
    target = slot_ids[:, None, :]
    offset = target - source + half_band
    inside = (offset >= 0) & (offset < band_count)
    column = jnp.clip(offset, 0, band_count - 1)
    keeping = inside & (pattern[source, column] == 1) & active[:, :, None] & active[:, None, :]
    picked = band_full[source, column]
    return jnp.where(keeping[:, :, :, None, None], picked, jnp.zeros((), picked.dtype))


def rotate(values, tile_set):
    return jnp.einsum("glpi,glmij->gmpj", values, tile_set, preferred_element_type=jnp.float32)


def local(orbitals, slot_ids, slot_count, band_tiles, pattern, occupation):
    all_rows = lax.all_gather(band_tiles, "dom", axis=2, tiled=True)
    tile_set = select_tiles(all_rows, pattern, slot_ids, slot_count)
    rotated_f = rotate(lax.all_gather(orbitals, "orb", axis=3, tiled=True), tile_set)
    rotated = rotated_f.astype(jnp.bfloat16)
    onehot = (
        slot_ids[:, :, None] == jnp.arange(occupation.shape[0], dtype=jnp.int32)[None, None, :]
    ).astype(jnp.float32)
    weights = jnp.einsum("glb,bj->glj", onehot, occupation, precision=lax.Precision.HIGHEST)
    widened = rotated.astype(jnp.float32)
    square = widened * widened
    partial_density = jnp.einsum("gmpj,gmj->gp", square, weights, precision=lax.Precision.HIGHEST)
    density = lax.psum(partial_density, "orb")
    return (rotated, density)


def solution(mesh):
    placed = (
        P("dom", None, None, "orb"),
        P("dom", None),
        P("dom"),
        P(None, None, "dom", "orb"),
        P(),
        P(None, "orb"),
    )
    return jax.shard_map(
        local,
        mesh=mesh,
        in_specs=placed,
        out_specs=(P("dom", None, None, "orb"), P("dom", None)),
        check_vma=False,
    )
```

profile of v0, /device:TPU:0, one launch (start us, length us, event | category | flops | bytes accessed | tf_op | source)
XLA Modules:
  0.0 198.5 jit_solution(10908176028303874434)
XLA Ops:
  7.2 0.0 copy-start
  7.2 0.0 copy-start.2
  7.2 0.0 copy-start.1
  7.2 0.0 copy-start.3
  7.2 0.0 all-gather.3.cloned.1.call-start
  7.3 0.7 all-gather.3.cloned.1.call-update
  7.9 0.0 all-gather.5.cloned.1.call-start
  8.0 0.7 all-gather.5.cloned.1.call-update
  8.7 0.7 fusion.26
  9.4 0.8 fusion.17
  10.2 0.1 reshape.76
  10.3 0.0 copy-done.1
  10.3 0.8 gather_fusion
  11.1 0.1 reshape.89
  11.2 0.0 copy-done.3
  11.2 0.1 iota_compare_fusion.2
  11.2 0.0 copy-done.2
  11.2 0.1 fusion.23
  11.3 0.1 copy.11
  11.4 0.0 copy-done
  11.4 0.2 fusion.13
  11.7 100.0 %all-gather.3.cloned.1.call-done = bf16[16,3,512,128]{3,2,1,0:T(8,128)(2,1)} async-done(((bf16[16,3,64,128]{3,2,1,0:T(8,128)(2,1)}), bf16[16,3,512,128]{3,2,1,0:T(8,128)(2,1)}) %all-gather.3.cloned.1.call-update) | async-done | bytes 6291472 | tf_op jit(solution)/shard_map/all_gather | solution.py:27
  111.7 5.8 %gather_fusion.1 = bf16[32,512,128]{2,1,0:T(8,128)(2,1)} fusion(bf16[16,3,512,128]{3,2,1,0:T(8,128)(2,1)} %all-gather.3.cloned.1.call-done, s32[32]{0:T(128)S(1)} %reshape.76), kind=kCustom, calls=%fused_computation.1 | custom fusion | bytes 8388864 | tf_op jit(solution)/shard_map/gather | solution.py:18
  117.5 7.6 %copy.12 = bf16[2,4,4,512,128]{3,4,1,2,0:T(8,128)(2,1)} copy(bf16[2,4,4,512,128]{4,3,2,1,0:T(8,128)(2,1)} %bitcast.27) | data formatting | bytes 8388608 | tf_op jit(solution)/shard_map/gather | solution.py:18
  125.1 45.7 %all-gather.5.cloned.1.call-done = bf16[2,4,1024,512]{3,2,1,0:T(8,128)(2,1)} async-done(((bf16[2,4,1024,128]{3,2,1,0:T(8,128)(2,1)}), bf16[2,4,1024,512]{3,2,1,0:T(8,128)(2,1)}) %all-gather.5.cloned.1.call-update) | async-done | bytes 8388624 | tf_op jit(solution)/shard_map/all_gather | solution.py:29
  170.8 9.2 %fusion.7 = bf16[2,4,1024,128]{2,3,1,0:T(8,128)(2,1)S(1)} fusion(bf16[2,4,1024,512]{3,2,1,0:T(8,128)(2,1)} %all-gather.5.cloned.1.call-done, bf16[2,4,4,512,128]{3,4,1,2,0:T(8,128)(2,1)} %copy.12, pred[2,4,4]{1,2,0:T(4,128)(4,1)S(1)} %copy.11), kind=kOutput, calls=%fused_computation.10 | convolution fusion | flops 4298113024 | bytes 14680096 | tf_op jit(solution)/shard_map/glpi,glmij->gmpj/dot_general | solution.py:23
  180.0 2.6 %copy.13 = bf16[2,4,1024,128]{3,2,1,0:T(8,128)(2,1)} copy(bf16[2,4,1024,128]{2,3,1,0:T(8,128)(2,1)S(1)} %fusion.7) | data formatting | bytes 4194304
  182.6 2.5 %fusion.2 = f32[2,1,1024,1]{2,1,3,0:T(1,128)S(1)} fusion(f32[2,4,128,1]{2,3,1,0:T(1,128)S(1)} %bitcast.29, bf16[2,4,1024,128]{2,3,1,0:T(8,128)(2,1)S(1)} %fusion.7), kind=kOutput, calls=%fused_computation.5 | convolution fusion | flops 14680064 | bytes 2109440 | tf_op jit(solution)/shard_map/gmpj,gmj->gp/dot_general | solution.py:37
  185.1 6.6 %psum.7 = f32[2,1024]{1,0:T(2,128)} all-reduce(f32[2,1024]{1,0:T(2,128)S(1)} %bitcast.28), channel_id=1, replica_groups=mesh['dom'=8,'orb'=4] {'orb'}, use_global_device_ids=true, to_apply=%region_0.1 | all-reduce | flops 2048 | bytes 16384 | tf_op jit(solution)/shard_map/psum | solution.py:38
  (2 shorter events, 0.0 us)
Async XLA Ops:
  7.2 4.3 %copy-start = (f32[16,128]{1,0:T(8,128)S(1)}, f32[16,128]{1,0:T(8,128)}, u32[]{:S(2)}) copy-start(f32[16,128]{1,0:T(8,128)} %param.11) | copy-start | bytes 24580
  7.2 4.1 %copy-start.2 = (s32[2,4]{1,0:T(2,128)S(1)}, s32[2,4]{1,0:T(2,128)}, u32[]{:S(2)}) copy-start(s32[2,4]{1,0:T(2,128)} %param.7) | copy-start | bytes 100
  7.2 3.1 %copy-start.1 = (s32[16,3]{0,1:T(4,128)S(1)}, s32[16,3]{0,1:T(4,128)}, u32[]{:S(2)}) copy-start(s32[16,3]{0,1:T(4,128)} %param.10) | copy-start | bytes 580
  7.2 4.0 %copy-start.3 = (s32[2]{0:T(128)S(1)}, s32[2]{0:T(128)}, u32[]{:S(2)}) copy-start(s32[2]{0:T(128)} %param.8) | copy-start | bytes 28
  7.2 104.4 %all-gather.3.cloned.1.call-start = ((), (), s32[]{:S(2)}) async-start(), calls=%async_computation | async-start | bytes 7077888 | tf_op jit(solution)/shard_map/all_gather | solution.py:27
  7.9 162.9 %all-gather.5.cloned.1.call-start = ((), (), s32[]{:S(2)}) async-start(), calls=%async_computation.1 | async-start | bytes 10485760 | tf_op jit(solution)/shard_map/all_gather | solution.py:29
Sparse Core Ops, SparseCore 0:
  10.2 101.4 all-gather.2
  113.2 57.5 all-gather.4
where the time goes:
time: 199 us; the launch traced here: 198 us
  waiting for transfers between devices  147 us (74%)
  local copies, waits for them, and re-layouts  17.1 us (9%)
  between operations  14.1 us (7%)
  matrix products  11.9 us (6%)
  blocking collectives  6.59 us (3%)
    all_gather x1, waiting for transfers between devices, local(): all_rows = lax.all_gather(band_tiles, 'dom', axis=2, tiled=True)  100 us
    all_gather x1, waiting for transfers between devices, local(): lax.all_gather(orbitals, 'orb', axis=3, tiled=True)  45.7 us
    gather x2, local copies, waits for them, and re-layouts, select_tiles(): picked = band_full[source, column]  13.4 us
    dot_general x1, matrix products, rotate(): jnp.einsum('glpi,glmij->gmpj', values, tile_set, preferred_element_type=j...  9.19 us
    psum x1, blocking collectives, local(): density = lax.psum(partial_density, 'orb')  6.59 us
  transfers between devices with their start and end apart: 2, of which 2 were waited for; matrix products, arithmetic and copies ran while one was open for 8% of the time, Pallas kernels for 0%

commit v1 on v0

v1 whole, which is shorter than its diff:
```python
import functools
import jax
import jax.numpy as jnp
from jax import lax
from jax.experimental import pallas as pl
from jax.experimental.pallas import tpu as pltpu
from jax.sharding import PartitionSpec as P

MESH = pl.DeviceIdType.MESH
CHUNKS = 4


def grid_of(mesh):
    devices = mesh.devices
    try:
        at = [tuple(d.coords) for d in devices[:, 0]]
        width = 1
        axis = [a != b for a, b in zip(at[0], at[1])].index(True)
        while width < len(at) and all(
            at[width][i] == at[0][i] + (width if i == axis else 0) for i in range(len(at[0]))
        ):
            width += 1
        first = tuple(devices[0, 0].coords)
        cores = sum(tuple(d.coords) == first for d in devices[0, :])
    except (AttributeError, IndexError, ValueError):
        width, cores = 1, 1
    if devices.shape[0] % width:
        width = 1
    if devices.shape[1] % cores:
        cores = 1
    return width, cores


def plan_chunks(total, height, width):
    first = (width - 1, (height - 1) * width)
    rest = ((width - 1) * height, height - 1)
    best = min(
        range(0, total),
        key=lambda n: max(first[i] * n + rest[i] * (total - n) for i in (0, 1)),
    ) if width > 1 else 0
    best = max(best, 1)
    chunks = [(0, best)]
    left, start = total - best, best
    for i in range(CHUNKS):
        count = left // CHUNKS + (1 if i < left % CHUNKS else 0)
        if count:
            chunks.append((start, count))
        start += count
    return chunks


def kernel(sizes, chunks, orb_hbm, tile_hbm, ids_ref, count_ref, pat_ref, occ_ref,
           out_ref, dens_ref, tiles, obuf, wcat, dbuf, acc_ref,
           own_sem, t_send, t_recv, o_send, o_recv, d_send, d_recv):
    height, width, chips, cores = sizes
    n_tile, n_dom, rows, cols = tiles.shape
    n_orb, n_blk, slots, points, _ = obuf.shape
    band = pat_ref.shape[1]
    half = (band - 1) // 2
    dom = lax.axis_index("dom")
    orb = lax.axis_index("orb")
    h, w = dom // width, dom % width
    x, core = orb // cores, orb % cores

    load_t = pltpu.make_async_copy(tile_hbm.at[pl.ds(half, n_tile)], tiles.at[:, dom], own_sem.at[0])
    load_t.start()
    load_o = pltpu.make_async_copy(orb_hbm, obuf.at[orb], own_sem.at[1])
    load_o.start()

    can = [h + 1 < height, h > 0, w + 1 < width, w > 0]
    to = [dom + width, dom - width, dom + 1, dom - 1]

    barrier = pltpu.get_barrier_semaphore()
    expect = n_orb - 1
    for d in range(4):
        @pl.when(can[d])
        def _(d=d):
            pl.semaphore_signal(barrier, inc=1, device_id={"dom": to[d]}, device_id_type=MESH)
        expect = expect + can[d].astype(jnp.int32)
    for d in range(1, n_orb):
        pl.semaphore_signal(barrier, inc=1, device_id={"orb": (orb + d) % n_orb}, device_id_type=MESH)
    pl.semaphore_wait(barrier, expect)
    load_t.wait()

    def tile_copy(c, origin, d):
        start, count = chunks[c]
        part = tiles.at[pl.ds(start, count), origin]
        return pltpu.make_async_remote_copy(
            src_ref=part, dst_ref=part, send_sem=t_send.at[d, c, origin],
            recv_sem=t_recv.at[c, origin], device_id={"dom": to[d]}, device_id_type=MESH)

    def forward(c, origin, dirs):
        for d in dirs:
            @pl.when(can[d])
            def _(d=d):
                tile_copy(c, origin, d).start()

    def settle(c, origin, dirs):
        for d in dirs:
            @pl.when(can[d])
            def _(d=d):
                tile_copy(c, origin, d).wait_send()

    def arrive(c, origin):
        tile_copy(c, origin, 0).wait_recv()

    def orb_copy(k, origin, target):
        part = obuf.at[origin, k // slots, k % slots]
        return pltpu.make_async_remote_copy(
            src_ref=part, dst_ref=part, send_sem=o_send.at[origin, target, k],
            recv_sem=o_recv.at[origin, k], device_id={"orb": target}, device_id_type=MESH)

    n_orb_chunk = n_blk * slots
    far = [((x + i) % chips) * cores + core for i in range(1, chips)]
    near = [x * cores + (core + i) % cores for i in range(1, cores)]

    n_chunk = len(chunks)
    for c in range(n_chunk):
        forward(c, dom, (2, 3, 0, 1) if c == 0 else (0, 1, 2, 3))
    load_o.wait()
    for k in range(n_orb_chunk):
        for target in far:
            orb_copy(k, orb, target).start()
    for k in range(n_orb_chunk):
        for target in near:
            orb_copy(k, orb, target).start()

    def relay_orb(k):
        for origin in far:
            orb_copy(k, origin, orb).wait_recv()
            for target in near:
                orb_copy(k, origin, target).start()

    def along_width(act_plus, act_minus):
        def step(u, carry):
            @pl.when(w - u >= 0)
            def _():
                act_plus(w - u)
            @pl.when(w + u < width)
            def _():
                act_minus(w + u)
            return carry
        lax.fori_loop(1, width, step, 0)

    def first_in(ow, d):
        arrive(0, h * width + ow)
        forward(0, h * width + ow, (d, 0, 1))

    along_width(lambda ow: first_in(ow, 2), lambda ow: first_in(ow, 3))

    n_rest = n_chunk - 1
    lag = 2

    def height_step(t, carry):
        sides = ((h - t >= 0, h - t, 0), (h + t < height, h + t, 1))
        for ok, row, d in sides:
            @pl.when(ok)
            def _(row=row, d=d):
                arrive(0, row * width + w)
                forward(0, row * width + w, (d,))
        for c in range(1, n_chunk):
            for ok, row, d in sides:
                @pl.when(ok)
                def _(row=row, d=d, c=c):
                    arrive(c, row * width + w)
                    forward(c, row * width + w, (d, 2, 3))
            k = (t - 1) * n_rest + (c - 1) - lag
            @pl.when((k >= 0) & (k < n_orb_chunk))
            def _(k=k):
                relay_orb(k)
        for ok, row, d in sides:
            def other(u, carry, row=row, d=d):
                origin = row * width + (w + u) % width
                arrive(0, origin)
                forward(0, origin, (d,))
                return carry
            @pl.when(ok)
            def _(other=other):
                lax.fori_loop(1, width, other, 0)
        return carry

    lax.fori_loop(1, height, height_step, 0)
    done = max(0, (height - 1) * n_rest - lag)
    for k in range(min(done, n_orb_chunk), n_orb_chunk):
        relay_orb(k)

    def late_row(i, carry):
        row = (h + i) % height
        for c in range(1, n_chunk):
            def late(ow, d, c=c):
                arrive(c, row * width + ow)
                forward(c, row * width + ow, (d,))
            along_width(functools.partial(late, d=2), functools.partial(late, d=3))
        return carry

    def orb_in(k, carry):
        for target in near:
            orb_copy(k, target, orb).wait_recv()
            for i in range(1, chips):
                origin = ((x + i) % chips) * cores + target % cores
                orb_copy(k, origin, orb).wait_recv()
        return carry
    lax.fori_loop(0, n_orb_chunk, orb_in, 0)
    lax.fori_loop(0, height, late_row, 0)

    zero = jnp.zeros((), jnp.bfloat16)
    for g in range(n_blk):
        ids = [ids_ref[g, m] for m in range(slots)]
        live = [count_ref[g] > m for m in range(slots)]
        for m0 in range(0, slots, 2):
            targets = [m for m in (m0, m0 + 1) if m < slots]
            sources = [l for l in range(slots) if any(abs(l - m) <= half for m in targets)]
            for si, l in enumerate(sources):
                for ti, m in enumerate(targets):
                    at = (pl.ds(si * n_dom * rows, n_dom * rows), pl.ds(ti * cols, cols))
                    if abs(l - m) > half:
                        wcat[at[0], at[1]] = jnp.zeros((n_dom * rows, cols), jnp.bfloat16)
                        continue
                    offset = ids[m] - ids[l] + half
                    column = jnp.clip(offset, 0, band - 1)
                    keep = (offset >= 0) & (offset < band) & live[l] & live[m] & (pat_ref[ids[l], column] == 1)
                    index = jnp.clip(ids[l] * band + column - half, 0, n_tile - 1)
                    picked = tiles[index].reshape(n_dom * rows, cols)
                    wcat[at[0], at[1]] = jnp.where(keep, picked, jnp.zeros_like(picked))
            depth = len(sources) * n_dom * rows
            block = min(256, points)

            def piece(i, carry, g=g, m0=m0, targets=targets, sources=sources, depth=depth):
                span = pl.ds(pl.multiple_of(i * block, block), block)
                lhs = jnp.concatenate(
                    [obuf[o, g, l, span, :] for l in sources for o in range(n_orb)], axis=1)
                both = jnp.dot(lhs, wcat[pl.ds(0, depth), :], preferred_element_type=jnp.float32)
                total = None
                for ti, m in enumerate(targets):
                    part = both[:, ti * cols:(ti + 1) * cols].astype(jnp.bfloat16)
                    out_ref[g, m, span, :] = part
                    wide = part.astype(jnp.float32)
                    term = wide * wide * occ_ref[pl.ds(ids_ref[g, m], 1), :]
                    total = term if total is None else total + term
                if m0 > 0:
                    total = total + acc_ref[span, :]
                acc_ref[span, :] = total
                return carry
            lax.fori_loop(0, points // block, piece, 0)
        ones = jnp.ones((8, cols), jnp.float32)
        line = lax.dot_general(ones, acc_ref[...], (((1,), (1,)), ((), ())),
                               precision=lax.Precision.HIGHEST, preferred_element_type=jnp.float32)
        dbuf[orb, pl.ds(g, 1), :] = line[0:1, :]

    def settle_all(origin, carry):
        row, ow = origin // width, origin % width
        for c in range(n_chunk):
            if c == 0:
                dirs = ((row <= h, 0), (row >= h, 1), ((row == h) & (ow <= w), 2), ((row == h) & (ow >= w), 3))
            else:
                dirs = (((ow == w) & (row <= h), 0), ((ow == w) & (row >= h), 1), (ow <= w, 2), (ow >= w, 3))
            for sent, d in dirs:
                @pl.when(sent & can[d])
                def _(c=c, d=d):
                    tile_copy(c, origin, d).wait_send()
        return carry
    lax.fori_loop(0, n_dom, settle_all, 0)

    def settle_orb(k, carry):
        for target in far + near:
            orb_copy(k, orb, target).wait_send()
        for origin in far:
            for target in near:
                orb_copy(k, origin, target).wait_send()
        return carry
    lax.fori_loop(0, n_orb_chunk, settle_orb, 0)

    def dens_copy(origin, target):
        return pltpu.make_async_remote_copy(
            src_ref=dbuf.at[origin], dst_ref=dbuf.at[origin], send_sem=d_send.at[target],
            recv_sem=d_recv.at[origin], device_id={"orb": target}, device_id_type=MESH)
    for i in range(1, n_orb):
        dens_copy(orb, (orb + i) % n_orb).start()
    for i in range(1, n_orb):
        dens_copy((orb + i) % n_orb, orb).wait_recv()
    total = dbuf[0]
    for o in range(1, n_orb):
        total = total + dbuf[o]
    dens_ref[...] = total
    for i in range(1, n_orb):
        dens_copy(orb, (orb + i) % n_orb).wait_send()


def solution(mesh):
    n_dom, n_orb = mesh.shape["dom"], mesh.shape["orb"]
    width, cores = grid_of(mesh)
    height, chips = n_dom // width, n_orb // cores

    def local(orbitals, slot_ids, slot_count, band_tiles, pattern, occupation):
        n_blk, slots, points, cols = orbitals.shape
        blocks, band, rows, _ = band_tiles.shape
        half = (band - 1) // 2
        n_tile = blocks * band - 2 * half
        chunks = plan_chunks(n_tile, height, width)
        n_k = n_blk * slots
        depth = min(slots, 2 * half + 2) * n_dom * rows
        dma = pltpu.SemaphoreType.DMA
        vmem = pl.BlockSpec(memory_space=pltpu.VMEM)
        smem = pl.BlockSpec(memory_space=pltpu.SMEM)
        hbm = pl.BlockSpec(memory_space=pltpu.HBM)
        return pl.pallas_call(
            functools.partial(kernel, (height, width, chips, cores), chunks),
            out_shape=(
                jax.ShapeDtypeStruct(orbitals.shape, jnp.bfloat16),
                jax.ShapeDtypeStruct((n_blk, points), jnp.float32),
            ),
            in_specs=[hbm, hbm, smem, smem, smem, vmem],
            out_specs=(vmem, vmem),
            scratch_shapes=[
                pltpu.VMEM((n_tile, n_dom, rows, cols), jnp.bfloat16),
                pltpu.VMEM((n_orb, n_blk, slots, points, cols), jnp.bfloat16),
                pltpu.VMEM((depth, 2 * cols), jnp.bfloat16),
                pltpu.VMEM((n_orb, n_blk, points), jnp.float32),
                pltpu.VMEM((points, cols), jnp.float32),
                dma((2,)),
                dma((4, len(chunks), n_dom)),
                dma((len(chunks), n_dom)),
                dma((n_orb, n_orb, n_k)),
                dma((n_orb, n_k)),
                dma((n_orb,)),
                dma((n_orb,)),
            ],
            compiler_params=pltpu.CompilerParams(
                collective_id=0, has_side_effects=True, vmem_limit_bytes=48 * 1024 * 1024),
        )(orbitals, band_tiles.reshape(blocks * band, rows, cols), slot_ids, slot_count, pattern, occupation)

    placed = (
        P("dom", None, None, "orb"),
        P("dom", None),
        P("dom"),
        P(None, None, "dom", "orb"),
        P(),
        P(None, "orb"),
    )
    return jax.shard_map(
        local,
        mesh=mesh,
        in_specs=placed,
        out_specs=(P("dom", None, None, "orb"), P("dom", None)),
        check_vma=False,
    )
```

time: 199 us -> 88.8 us (0.45)
  waiting for transfers between devices: 147 us -> 0 us
  Pallas kernels: 0 us -> 80.4 us
  between operations: 14.1 us -> 0.64 us
  matrix products: 11.9 us -> 0 us
  local copies, waits for them, and re-layouts: 17.1 us -> 7.43 us
  blocking collectives: 6.59 us -> 0 us
    all_gather x2 -> x0, waiting for transfers between devices: 146 us -> none  [the longest x1 100 us: local(): all_rows = lax.all_gather(band_tiles, 'dom', axis=2, tiled=True)]
    pallas_call x0 -> x1, Pallas kernels: none -> 80.4 us  [local(): pl.pallas_call(functools.partial(kernel, (height, width, chips, cores), c...]
    gather x3 -> x0, local copies, waits for them, and re-layouts: 14.2 us -> none  [the longest x2 13.4 us: select_tiles(): picked = band_full[source, column]]
    dot_general x3 -> x0, matrix products: 11.9 us -> none  [the longest x1 9.19 us: rotate(): jnp.einsum('glpi,glmij->gmpj', values, tile_set, preferred_element_type=j...]
    psum x1 -> x0, blocking collectives: 6.59 us -> none  [local(): density = lax.psum(partial_density, 'orb')]
    unnamed x9 -> x13, local copies, waits for them, and re-layouts: 2.58 us -> 7.43 us
  transfers between devices with their start and end apart: 2 -> 0, of which waited for: 2 -> 0; matrix products, arithmetic and copies ran while one was open for 8% -> 0% of each run, Pallas kernels for 0% -> 0%
where the time goes in v1:
time: 88.8 us; the launch traced here: 88.5 us
  Pallas kernels  80.4 us (91%)
  local copies, waits for them, and re-layouts  7.43 us (8%)
    pallas_call x1, Pallas kernels, local(): pl.pallas_call(functools.partial(kernel, (height, width, chips, cores), c...  80.4 us
    unnamed x13, local copies, waits for them, and re-layouts  7.43 us

profile of v1, /device:TPU:0, one launch (start us, length us, event | category | flops | bytes accessed | tf_op | source)
XLA Modules:
  0.0 88.5 jit_solution(4033905598886284656)
XLA Ops:
  0.6 0.8 copy.8.pat_ref
  1.4 0.0 copy-start
  1.4 1.6 %copy-done = bf16[2,4,1024,128]{3,2,1,0:T(8,128)(2,1)S(1)} copy-done((bf16[2,4,1024,128]{3,2,1,0:T(8,128)(2,1)S(1)}, bf16[2,4,1024,128]{3,2,1,0:T(8,128)(2,1)}, u32[]{:S(2)}) %copy-start) | copy-done | bytes 2097176
  3.0 0.0 copy-start.1
  3.0 1.1 %copy-done.1 = bf16[16,3,64,128]{3,2,1,0:T(8,128)(2,1)S(1)} copy-done((bf16[16,3,64,128]{3,2,1,0:T(8,128)(2,1)S(1)}, bf16[16,3,64,128]{3,2,1,0:T(8,128)(2,1)}, u32[]{:S(2)}) %copy-start.1) | copy-done | bytes 786456
  4.1 0.0 copy-start.2
  4.1 0.7 copy-done.2
  4.8 0.0 copy-start.3
  4.8 0.7 copy-done.3
  5.5 0.0 copy-start.4
  5.5 0.7 copy-done.4
  6.1 80.4 %shard_map.77 = (bf16[2,4,1024,128]{3,2,1,0:T(8,128)(2,1)S(1)}, f32[2,1024]{1,0:T(2,128)S(1)}) custom-call(bf16[2,4,1024,128]{3,2,1,0:T(8,128)(2,1)S(1)} %copy-done, bf16[48,64,128]{2,1,0:T(8,128)(2,1)S(1)} %bitcast.1, s32[2,4]{1,0:T(2,128)S(1)} %copy-done.3, s32[2]{0:T(128)S(1)} %copy-done.4, s32[16,3]{1,0:T(8,128)S(1)} %copy.8.pat_ref, f32[16,128]{1,0:T(8,128)S(1)} %copy-done.2), custom_call_target="tpu_custom_call" | custom-call | tf_op jit(solution)/shard_map/pallas_call | solution.py:306
  86.6 1.3 %copy.11 = bf16[2,4,1024,128]{3,2,1,0:T(8,128)(2,1)} copy(bf16[2,4,1024,128]{3,2,1,0:T(8,128)(2,1)S(1)} %get-tuple-element.4) | data formatting | bytes 4194304
  87.9 0.6 copy.12
Async XLA Ops:
  1.4 1.6 %copy-start = (bf16[2,4,1024,128]{3,2,1,0:T(8,128)(2,1)S(1)}, bf16[2,4,1024,128]{3,2,1,0:T(8,128)(2,1)}, u32[]{:S(2)}) copy-start(bf16[2,4,1024,128]{3,2,1,0:T(8,128)(2,1)} %orb_hbm.1) | copy-start | bytes 6291460
  3.0 1.1 %copy-start.1 = (bf16[16,3,64,128]{3,2,1,0:T(8,128)(2,1)S(1)}, bf16[16,3,64,128]{3,2,1,0:T(8,128)(2,1)}, u32[]{:S(2)}) copy-start(bf16[16,3,64,128]{3,2,1,0:T(8,128)(2,1)} %param.9) | copy-start | bytes 2359300
  4.1 0.7 copy-start.2
  4.8 0.7 copy-start.3
  5.5 0.7 copy-start.4

commit v2 on v1

--- a/solution.py
+++ b/solution.py
@@ -53,16 +53,16 @@
            out_ref, dens_ref, tiles, obuf, wcat, dbuf, acc_ref,
            own_sem, t_send, t_recv, o_send, o_recv, d_send, d_recv):
     height, width, chips, cores = sizes
-    n_tile, n_dom, rows, cols = tiles.shape
+    n_dom, n_tile, rows, cols = tiles.shape
     n_orb, n_blk, slots, points, _ = obuf.shape
-    band = pat_ref.shape[1]
+    band = pat_ref.shape[0]
     half = (band - 1) // 2
     dom = lax.axis_index("dom")
     orb = lax.axis_index("orb")
     h, w = dom // width, dom % width
     x, core = orb // cores, orb % cores
 
-    load_t = pltpu.make_async_copy(tile_hbm.at[pl.ds(half, n_tile)], tiles.at[:, dom], own_sem.at[0])
+    load_t = pltpu.make_async_copy(tile_hbm.at[pl.ds(half, n_tile)], tiles.at[dom], own_sem.at[0])
     load_t.start()
     load_o = pltpu.make_async_copy(orb_hbm, obuf.at[orb], own_sem.at[1])
     load_o.start()
@@ -84,7 +84,7 @@
 
     def tile_copy(c, origin, d):
         start, count = chunks[c]
-        part = tiles.at[pl.ds(start, count), origin]
+        part = tiles.at[origin, pl.ds(start, count)]
         return pltpu.make_async_remote_copy(
             src_ref=part, dst_ref=part, send_sem=t_send.at[d, c, origin],
             recv_sem=t_recv.at[c, origin], device_id={"dom": to[d]}, device_id_type=MESH)
@@ -218,12 +218,12 @@
                         continue
                     offset = ids[m] - ids[l] + half
                     column = jnp.clip(offset, 0, band - 1)
-                    keep = (offset >= 0) & (offset < band) & live[l] & live[m] & (pat_ref[ids[l], column] == 1)
+                    keep = (offset >= 0) & (offset < band) & live[l] & live[m] & (pat_ref[column, ids[l]] == 1)
                     index = jnp.clip(ids[l] * band + column - half, 0, n_tile - 1)
-                    picked = tiles[index].reshape(n_dom * rows, cols)
+                    picked = tiles[:, index].reshape(n_dom * rows, cols)
                     wcat[at[0], at[1]] = jnp.where(keep, picked, jnp.zeros_like(picked))
             depth = len(sources) * n_dom * rows
-            block = min(256, points)
+            block = min(1024, points)
 
             def piece(i, carry, g=g, m0=m0, targets=targets, sources=sources, depth=depth):
                 span = pl.ds(pl.multiple_of(i * block, block), block)
@@ -306,13 +306,13 @@
         return pl.pallas_call(
             functools.partial(kernel, (height, width, chips, cores), chunks),
             out_shape=(
-                jax.ShapeDtypeStruct(orbitals.shape, jnp.bfloat16),
-                jax.ShapeDtypeStruct((n_blk, points), jnp.float32),
+                pltpu.VMEM(orbitals.shape, jnp.bfloat16),
+                pltpu.VMEM((n_blk, points), jnp.float32),
             ),
             in_specs=[hbm, hbm, smem, smem, smem, vmem],
             out_specs=(vmem, vmem),
             scratch_shapes=[
-                pltpu.VMEM((n_tile, n_dom, rows, cols), jnp.bfloat16),
+                pltpu.VMEM((n_dom, n_tile, rows, cols), jnp.bfloat16),
                 pltpu.VMEM((n_orb, n_blk, slots, points, cols), jnp.bfloat16),
                 pltpu.VMEM((depth, 2 * cols), jnp.bfloat16),
                 pltpu.VMEM((n_orb, n_blk, points), jnp.float32),
@@ -326,8 +326,8 @@
                 dma((n_orb,)),
             ],
             compiler_params=pltpu.CompilerParams(
-                collective_id=0, has_side_effects=True, vmem_limit_bytes=48 * 1024 * 1024),
-        )(orbitals, band_tiles.reshape(blocks * band, rows, cols), slot_ids, slot_count, pattern, occupation)
+                collective_id=0, has_side_effects=True, vmem_limit_bytes=60 * 1024 * 1024),
+        )(orbitals, band_tiles.reshape(blocks * band, rows, cols), slot_ids, slot_count, pattern.T, occupation)
 
     placed = (
         P("dom", None, None, "orb"),

time: 88.8 us -> 80.2 us (0.903)
  local copies, waits for them, and re-layouts: 7.43 us -> 1.92 us
  Pallas kernels: 80.4 us -> 77.4 us
    unnamed x13 -> x2, local copies, waits for them, and re-layouts: 7.43 us -> 1.92 us
    pallas_call x1, Pallas kernels: 80.4 us -> 77.4 us  [local(): pl.pallas_call(functools.partial(kernel, (height, width, chips, cores), c...]
where the time goes in v2:
time: 80.2 us; the launch traced here: 79.9 us
  Pallas kernels  77.4 us (97%)
  local copies, waits for them, and re-layouts  1.92 us (2%)
    pallas_call x1, Pallas kernels, local(): pl.pallas_call(functools.partial(kernel, (height, width, chips, cores), c...  77.4 us
    unnamed x2, local copies, waits for them, and re-layouts  1.92 us

profile of v2, /device:TPU:0, one launch (start us, length us, event | category | flops | bytes accessed | tf_op | source)
XLA Modules:
  0.0 79.9 jit_solution(7461252653680339056)
XLA Ops:
  0.6 77.4 %shard_map.77 = (bf16[2,4,1024,128]{3,2,1,0:T(8,128)(2,1)S(1)}, f32[2,1024]{1,0:T(2,128)S(1)}) custom-call(bf16[2,4,1024,128]{3,2,1,0:T(8,128)(2,1)} %orb_hbm.1, bf16[48,64,128]{2,1,0:T(8,128)(2,1)} %bitcast.2, s32[2,4]{1,0:T(2,128)} %ids_ref.1, s32[2]{0:T(128)} %count_ref.1, s32[3,16]{1,0:T(4,128)} %bitcast.3, f32[16,128]{1,0:T(8,128)} %occ_ref.1), custom_call_target="tpu_custom_call" | custom-call | tf_op jit(solution)/shard_map/pallas_call | solution.py:306
  78.0 1.3 %copy.10 = bf16[2,4,1024,128]{3,2,1,0:T(8,128)(2,1)} copy(bf16[2,4,1024,128]{3,2,1,0:T(8,128)(2,1)S(1)} %get-tuple-element.2) | data formatting | bytes 4194304
  79.3 0.6 copy.11

commit v3 on v2

--- a/solution.py
+++ b/solution.py
@@ -208,28 +208,29 @@
         ids = [ids_ref[g, m] for m in range(slots)]
         live = [count_ref[g] > m for m in range(slots)]
         for m0 in range(0, slots, 2):
+            slot = g * ((slots + 1) // 2) + m0 // 2
             targets = [m for m in (m0, m0 + 1) if m < slots]
             sources = [l for l in range(slots) if any(abs(l - m) <= half for m in targets)]
             for si, l in enumerate(sources):
                 for ti, m in enumerate(targets):
                     at = (pl.ds(si * n_dom * rows, n_dom * rows), pl.ds(ti * cols, cols))
                     if abs(l - m) > half:
-                        wcat[at[0], at[1]] = jnp.zeros((n_dom * rows, cols), jnp.bfloat16)
+                        wcat[slot, at[0], at[1]] = jnp.zeros((n_dom * rows, cols), jnp.bfloat16)
                         continue
                     offset = ids[m] - ids[l] + half
                     column = jnp.clip(offset, 0, band - 1)
                     keep = (offset >= 0) & (offset < band) & live[l] & live[m] & (pat_ref[column, ids[l]] == 1)
                     index = jnp.clip(ids[l] * band + column - half, 0, n_tile - 1)
                     picked = tiles[:, index].reshape(n_dom * rows, cols)
-                    wcat[at[0], at[1]] = jnp.where(keep, picked, jnp.zeros_like(picked))
+                    wcat[slot, at[0], at[1]] = jnp.where(keep, picked, jnp.zeros_like(picked))
             depth = len(sources) * n_dom * rows
             block = min(1024, points)
 
-            def piece(i, carry, g=g, m0=m0, targets=targets, sources=sources, depth=depth):
-                span = pl.ds(pl.multiple_of(i * block, block), block)
+            def piece(i, carry, g=g, m0=m0, targets=targets, sources=sources, depth=depth, slot=slot):
+                span = pl.ds(0 if points == block else pl.multiple_of(i * block, block), block)
                 lhs = jnp.concatenate(
                     [obuf[o, g, l, span, :] for l in sources for o in range(n_orb)], axis=1)
-                both = jnp.dot(lhs, wcat[pl.ds(0, depth), :], preferred_element_type=jnp.float32)
+                both = jnp.dot(lhs, wcat[slot, pl.ds(0, depth), :], preferred_element_type=jnp.float32)
                 total = None
                 for ti, m in enumerate(targets):
                     part = both[:, ti * cols:(ti + 1) * cols].astype(jnp.bfloat16)
@@ -241,7 +242,10 @@
                     total = total + acc_ref[span, :]
                 acc_ref[span, :] = total
                 return carry
-            lax.fori_loop(0, points // block, piece, 0)
+            if points == block:
+                piece(0, 0)
+            else:
+                lax.fori_loop(0, points // block, piece, 0)
         ones = jnp.ones((8, cols), jnp.float32)
         line = lax.dot_general(ones, acc_ref[...], (((1,), (1,)), ((), ())),
                                precision=lax.Precision.HIGHEST, preferred_element_type=jnp.float32)
@@ -314,7 +318,7 @@
             scratch_shapes=[
                 pltpu.VMEM((n_dom, n_tile, rows, cols), jnp.bfloat16),
                 pltpu.VMEM((n_orb, n_blk, slots, points, cols), jnp.bfloat16),
-                pltpu.VMEM((depth, 2 * cols), jnp.bfloat16),
+                pltpu.VMEM((n_blk * ((slots + 1) // 2), depth, 2 * cols), jnp.bfloat16),
                 pltpu.VMEM((n_orb, n_blk, points), jnp.float32),
                 pltpu.VMEM((points, cols), jnp.float32),
                 dma((2,)),

time: 80.2 us -> 80.2 us (level)
  no operation moved by 1% of the time
where the time goes in v3:
time: 80.2 us; the launch traced here: 79.9 us
  Pallas kernels  77.4 us (97%)
  local copies, waits for them, and re-layouts  1.92 us (2%)
    pallas_call x1, Pallas kernels, local(): pl.pallas_call(functools.partial(kernel, (height, width, chips, cores), c...  77.4 us
    unnamed x2, local copies, waits for them, and re-layouts  1.92 us

profile of v3, /device:TPU:0, one launch (start us, length us, event | category | flops | bytes accessed | tf_op | source)
XLA Modules:
  0.0 79.9 jit_solution(2037523344661281959)
XLA Ops:
  0.6 77.4 %shard_map.77 = (bf16[2,4,1024,128]{3,2,1,0:T(8,128)(2,1)S(1)}, f32[2,1024]{1,0:T(2,128)S(1)}) custom-call(bf16[2,4,1024,128]{3,2,1,0:T(8,128)(2,1)} %orb_hbm.1, bf16[48,64,128]{2,1,0:T(8,128)(2,1)} %bitcast.2, s32[2,4]{1,0:T(2,128)} %ids_ref.1, s32[2]{0:T(128)} %count_ref.1, s32[3,16]{1,0:T(4,128)} %bitcast.3, f32[16,128]{1,0:T(8,128)} %occ_ref.1), custom_call_target="tpu_custom_call" | custom-call | tf_op jit(solution)/shard_map/pallas_call | solution.py:310
  78.0 1.3 %copy.10 = bf16[2,4,1024,128]{3,2,1,0:T(8,128)(2,1)} copy(bf16[2,4,1024,128]{3,2,1,0:T(8,128)(2,1)S(1)} %get-tuple-element.2) | data formatting | bytes 4194304
  79.3 0.6 copy.11
